TPU v7x, 32 devices: a whole 2x2x4 slice. The times are simulated.
32 devices in a mesh: spin: 2 (over x), band: 16 (over z, y, core).
Axes of the slice: x: 2, y: 2, z: 4, core: 2. Of those that a mesh axis runs over, the one named last changes fastest.
Arguments:
- orbitals: bfloat16 [32, 262144], P(('spin', 'band')), parts along dimension 0, may hold values from -6 to 6
- trial: bfloat16 [32, 262144], P(('spin', 'band')), parts along dimension 0, may hold values from -6 to 6
- occupations: int32 [32], P(('spin', 'band')), parts along dimension 0, may hold values 0 or 1
Outputs:
- exchange: bfloat16 [32, 262144], P(('spin', 'band')), parts along dimension 0
- projected: bfloat16 [32, 262144], P('spin', 'band'), parts along dimension 0
There are 2 independent parts, one for each index of `spin`. A program takes and returns all parts, laid end to end along the dimension named above; each array names one. Nothing has to cross between parts.
All inputs are finite; a program needn't handle non-finite values. No bound on the sum of `occupations` on one device may be relied on, other than what follows from the above.
Results may differ from a plain program's by a relative error of at most 0.018.
Values may be sent and summed in bfloat16 or wider, within the bound.
A program may use at most 64 MiB of HBM per device.

v0:
```python
import functools
import math

import jax
import jax.numpy as jnp
from jax import lax
from jax.experimental import pallas as pl
from jax.experimental.pallas import tpu as pltpu
from jax.sharding import PartitionSpec as P

NG = 64
FRACTION = 0.25
OMEGA = 1.0
CHUNK = 2048
MESH = pl.DeviceIdType.MESH


def passed_along(value, axis, steps):
    count = lax.axis_size(axis)
    pairs = [(source, (source + steps) % count) for source in range(count)]
    return lax.ppermute(value, axis, pairs)


def cas_table(extent):
    indices = jnp.arange(extent, dtype=jnp.int32)
    products = indices[:, None] * indices[None, :] % extent
    phases = products.astype(jnp.float32) * (2.0 * math.pi / extent)
    return (jnp.cos(phases) + jnp.sin(phases)).astype(jnp.bfloat16)


def screened_kernel(extent):
    modes = jnp.arange(extent, dtype=jnp.int32)
    modes = jnp.where(2 * modes < extent, modes, modes - extent)
    wavenum = modes.astype(jnp.float32) * (2.0 * math.pi / extent)
    squares = wavenum * wavenum
    norm_sq = squares[:, None, None] + squares[None, :, None] + squares[None, None, :]
    bounded = jnp.where(norm_sq > 0, norm_sq, 1.0)
    screened = jnp.where(
        norm_sq > 0,
        4.0 * math.pi / bounded * (1.0 - jnp.exp(-bounded / (4.0 * OMEGA * OMEGA))),
        math.pi / (OMEGA * OMEGA),
    )
    return screened / extent**3


def screened_potential(values, table, kernel):
    patterns = ("ga,abc->gbc", "gb,abc->agc", "gc,abc->abg")
    for pattern in patterns:
        values = jnp.einsum(pattern, table, values, preferred_element_type=jnp.float32).astype(
            jnp.bfloat16
        )
    values = (values.astype(jnp.float32) * kernel).astype(jnp.bfloat16)
    for ordinal, pattern in enumerate(patterns):
        values = jnp.einsum(pattern, table, values, preferred_element_type=jnp.float32)
        if ordinal < 2:
            values = values.astype(jnp.bfloat16)
    return values


def greet(count, me):
    barrier = pltpu.get_barrier_semaphore()

    @pl.loop(1, count)
    def _(step):
        peer = lax.rem(me + step, count)
        pl.semaphore_signal(barrier, inc=1, device_id={"band": peer}, device_id_type=MESH)

    pl.semaphore_wait(barrier, count - 1)


def slabs_body(count, arrays, *refs):
    ins, outs = refs[:arrays], refs[arrays : 2 * arrays]
    send_sem, recv_sem, own_sem = refs[2 * arrays :]
    me = lax.axis_index("band")
    greet(count, me)

    def remote(which, peer, slot):
        return pltpu.make_async_remote_copy(
            src_ref=ins[which].at[peer],
            dst_ref=outs[which].at[slot],
            send_sem=send_sem.at[which, peer],
            recv_sem=recv_sem.at[which, slot],
            device_id={"band": peer},
            device_id_type=MESH,
        )

    def own(which):
        return pltpu.make_async_copy(ins[which].at[me], outs[which].at[me], own_sem.at[which])

    for which in range(arrays):

        @pl.loop(1, count)
        def _(step):
            remote(which, lax.rem(me + step, count), me).start()

        own(which).start()
    for which in range(arrays):
        own(which).wait()

        @pl.loop(1, count)
        def _(step):
            remote(which, lax.rem(me + step, count), me).wait_send()

        @pl.loop(1, count)
        def _(step):
            peer = lax.rem(me + count - step, count)
            remote(which, peer, peer).wait_recv()


def to_slabs(arrays, collective_id):
    count = lax.axis_size("band")
    number = len(arrays)
    shape = arrays[0].shape
    size = math.prod(shape)
    return pl.pallas_call(
        functools.partial(slabs_body, count, number),
        out_shape=[jax.ShapeDtypeStruct(shape, a.dtype) for a in arrays],
        in_specs=[pl.BlockSpec(memory_space=pltpu.VMEM)] * number,
        out_specs=[pl.BlockSpec(memory_space=pltpu.VMEM)] * number,
        scratch_shapes=[
            pltpu.SemaphoreType.DMA((number, count)),
            pltpu.SemaphoreType.DMA((number, count)),
            pltpu.SemaphoreType.DMA((number,)),
        ],
        cost_estimate=pl.CostEstimate(
            flops=0, bytes_accessed=size * 40 * number, transcendentals=0
        ),
        compiler_params=pltpu.CompilerParams(
            collective_id=collective_id, has_side_effects=True
        ),
        name="to_slabs",
    )(*arrays)


def summed_body(count, part_ref, total_ref, parts, send_sem, recv_sem):
    me = lax.axis_index("band")
    greet(count, me)

    def remote(peer, slot):
        return pltpu.make_async_remote_copy(
            src_ref=part_ref,
            dst_ref=parts.at[slot],
            send_sem=send_sem.at[peer],
            recv_sem=recv_sem.at[slot],
            device_id={"band": peer},
            device_id_type=MESH,
        )

    @pl.loop(1, count)
    def _(step):
        remote(lax.rem(me + step, count), me).start()

    parts[pl.ds(me, 1)] = part_ref[...][None]

    @pl.loop(1, count)
    def _(step):
        remote(lax.rem(me + step, count), me).wait_send()

    @pl.loop(1, count)
    def _(step):
        peer = lax.rem(me + count - step, count)
        remote(peer, peer).wait_recv()

    total_ref[...] = jnp.sum(parts[...], axis=0)


def summed(part, collective_id):
    count = lax.axis_size("band")
    return pl.pallas_call(
        functools.partial(summed_body, count),
        out_shape=jax.ShapeDtypeStruct(part.shape, part.dtype),
        in_specs=[pl.BlockSpec(memory_space=pltpu.VMEM)],
        out_specs=pl.BlockSpec(memory_space=pltpu.VMEM),
        scratch_shapes=[
            pltpu.VMEM((count,) + part.shape, part.dtype),
            pltpu.SemaphoreType.DMA((count,)),
            pltpu.SemaphoreType.DMA((count,)),
        ],
        compiler_params=pltpu.CompilerParams(
            collective_id=collective_id, has_side_effects=True
        ),
        name="summed",
    )(part)


def rows_body(chunk, *refs):
    half = len(refs) // 2
    for line, rows in zip(refs[:half], refs[half:]):

        @pl.loop(0, line.shape[1] // chunk, unroll=4)
        def _(step):
            cut = pl.ds(pl.multiple_of(step * chunk, chunk), chunk)
            out = pl.ds(pl.multiple_of(step * (chunk // 128), chunk // 128), chunk // 128)
            wide = line[:, cut].astype(jnp.float32).reshape(chunk // 128, 128)
            rows[out, :] = wide.astype(rows.dtype)


def as_rows(*lines):
    number = len(lines)
    cells = lines[0].shape[1]
    return pl.pallas_call(
        functools.partial(rows_body, CHUNK),
        out_shape=[jax.ShapeDtypeStruct((cells // 128, 128), a.dtype) for a in lines],
        in_specs=[pl.BlockSpec(memory_space=pltpu.VMEM)] * number,
        out_specs=[pl.BlockSpec(memory_space=pltpu.VMEM)] * number,
        cost_estimate=pl.CostEstimate(
            flops=0, bytes_accessed=cells * 16 * number, transcendentals=0
        ),
        name="as_rows",
    )(*lines)


def local(orbitals, trial, occupations):
    count = lax.axis_size("band")
    cells = orbitals.shape[1]
    extent = NG
    table = cas_table(extent)
    kernel = screened_kernel(extent)
    cube = (extent, extent, extent)
    fill = occupations.astype(jnp.bfloat16)

    (lined,) = as_rows(orbitals)
    (trial_rows,) = as_rows(trial)
    visitor, visitor_fill = passed_along((lined, fill), "band", 1)
    own = lined.reshape(cube).astype(jnp.float32)
    own_weighted = own * fill[0].astype(jnp.float32)
    own_potential = screened_potential((own * own).astype(jnp.bfloat16), table, kernel)
    accumulated = own_potential * own_weighted

    other = visitor.reshape(cube).astype(jnp.float32)
    potential = screened_potential((own * other).astype(jnp.bfloat16), table, kernel)
    carried = passed_along((potential * own_weighted).astype(jnp.bfloat16), "band", -1)
    accumulated = accumulated + potential * (other * visitor_fill[0].astype(jnp.float32))
    accumulated = accumulated + carried.astype(jnp.float32)
    exchange = (-FRACTION * accumulated).astype(jnp.bfloat16).reshape(1, cells)

    slab = (count, cells // count // 128, 128)
    grid_exchange, grid_trial = to_slabs((exchange.reshape(slab), trial_rows.reshape(slab)), 1)
    grid_exchange = grid_exchange.reshape(count, -1)
    grid_trial = grid_trial.reshape(count, -1)
    part = lax.dot_general(
        grid_exchange, grid_trial, (((1,), (1,)), ((), ())), preferred_element_type=jnp.float32
    )
    intersection_low = (summed(part, 2) / math.sqrt(cells)).astype(jnp.bfloat16)
    projected = -(
        lax.dot_general(
            intersection_low,
            grid_exchange,
            (((0,), (0,)), ((), ())),
            preferred_element_type=jnp.float32,
        )
        / math.sqrt(count)
    )
    return (exchange, projected.astype(jnp.bfloat16))


def solution(mesh):
    return jax.shard_map(
        local,
        mesh=mesh,
        in_specs=(P(("spin", "band"), None), P(("spin", "band"), None), P(("spin", "band"))),
        out_specs=(P(("spin", "band"), None), P("spin", "band")),
        check_vma=False,
    )
```

profile of v0, /device:TPU:0, one launch (start us, length us, event | category | flops | bytes accessed | tf_op | source)
XLA Modules:
  0.0 96.8 jit_solution(2446618162544193886)
XLA Ops:
  0.6 2.4 %as_rows.2 = bf16[2048,128]{1,0:T(8,128)(2,1)} custom-call(bf16[1,262144]{1,0:T(2,128)(2,1)} %refs_0_.2), custom_call_target="tpu_custom_call" | custom-call | bytes 4194304 | tf_op jit(solution)/shard_map/as_rows/pallas_call | solution.py:201
  4.2 3.6 %collective-permute-start.1 = (bf16[1]{0:T(256)(128)(2,1)}, bf16[1]{0:T(256)(128)(2,1)}, u32[]{:S(2)}, u32[]{:S(2)}) collective-permute-start(bf16[1]{0:T(256)(128)(2,1)} %convert_element_type.186), channel_id=1, source_target_pairs={{0,1},{1,2},{2,3},{3,4},{4,5},{5,6},{6,7},{7,8},{8,9},{9,10},{10,1... | collective-permute-start | bytes 14 | tf_op jit(solution)/shard_map/ppermute | solution.py:21
  7.8 2.4 %as_rows.3 = bf16[2048,128]{1,0:T(8,128)(2,1)} custom-call(bf16[1,262144]{1,0:T(2,128)(2,1)} %refs_0_.3), custom_call_target="tpu_custom_call" | custom-call | bytes 4194304 | tf_op jit(solution)/shard_map/as_rows/pallas_call | solution.py:201
  10.3 5.4 %collective-permute-done.1 = bf16[1]{0:T(256)(128)(2,1)} collective-permute-done((bf16[1]{0:T(256)(128)(2,1)}, bf16[1]{0:T(256)(128)(2,1)}, u32[]{:S(2)}, u32[]{:S(2)}) %collective-permute-start.1) | collective-permute-done | bytes 34 | tf_op jit(solution)/shard_map/ppermute | solution.py:21
  16.3 2.5 %fusion.16 = (bf16[2048,128]{1,0:T(8,128)(2,1)}, f32[2048,128]{1,0:T(8,128)}, bf16[2048,128]{1,0:T(8,128)(2,1)S(1)}, f32[2048,128]{1,0:T(8,128)S(1)}) fusion(bf16[2048,128]{1,0:T(8,128)(2,1)} %as_rows.2, f32[]{:T(128)S(6)} %convert.2, bf16[2048,128]{1,0:T(8,128)(2,1)S(1)} %collective-permute-done, f32[]{:T(128)S(6)} %convert.3), kind=kLoop, calls=%fused_computation.38 | loop fusion | flops 2097152 | bytes 4194312 | tf_op jit(solution)/shard_map/convert_element_type | solution.py:227
  19.2 1.0 %fusion.20 = bf16[64,64,64]{2,0,1:T(8,128)(2,1)S(1)} fusion(bf16[64,64,64]{2,1,0:T(8,128)(2,1)S(1)} %convert_element_type.191), kind=kOutput, calls=%fused_computation.42 | convolution fusion | flops 33619968 | bytes 1048576 | tf_op jit(solution)/shard_map/ga,abc->gbc/dot_general | solution.py:49
  20.2 2.2 %multiply_convert_fusion.2 = bf16[64,64,64]{2,1,0:T(8,128)(2,1)S(1)} fusion(bf16[64,64,64]{2,0,1:T(8,128)(2,1)S(1)} %fusion.20, f32[64]{0:T(128)S(1)} %fusion.88, f32[64,64]{1,0:T(8,128)S(1)} %broadcast_add_fusion), kind=kOutput, calls=%fused_computation.19 | convolution fusion | flops 71172096 | bytes 1065216 | tf_op jit(solution)/shard_map/gc,abc->abg/dot_general | solution.py:49
  22.3 2.0 %fusion.18 = bf16[64,64,64]{2,0,1:T(8,128)(2,1)} fusion(bf16[64,64,64]{2,1,0:T(8,128)(2,1)S(1)} %multiply_convert_fusion.2), kind=kOutput, calls=%fused_computation.40 | convolution fusion | flops 33619968 | bytes 1048576 | tf_op jit(solution)/shard_map/ga,abc->gbc/dot_general | solution.py:54
  24.4 1.6 %mul.231 = f32[64,64,64]{2,1,0:T(8,128)S(1)} reshape(f32[2048,128]{1,0:T(8,128)} %get-tuple-element.7) | data formatting | bytes 2097152 | tf_op jit(solution)/shard_map/mul | solution.py:226
  25.9 4.2 %multiply_convert_fusion.1 = (bf16[64,64,64]{2,1,0:T(8,128)(2,1)}, f32[64,64,64]{2,1,0:T(8,128)}) fusion(f32[64,64,64]{2,1,0:T(8,128)S(1)} %mul.231, bf16[64,64,64]{2,0,1:T(8,128)(2,1)} %fusion.18), kind=kOutput, calls=%fused_computation.18 | convolution fusion | flops 68026368 | bytes 3145728 | tf_op jit(solution)/shard_map/gc,abc->abg/dot_general | solution.py:54
  30.1 1.8 %collective-permute-start.2 = (bf16[64,64,64]{2,1,0:T(8,128)(2,1)}, bf16[64,64,64]{2,1,0:T(8,128)(2,1)}, u32[]{:S(2)}, u32[]{:S(2)}) collective-permute-start(bf16[64,64,64]{2,1,0:T(8,128)(2,1)} %get-tuple-element.10), channel_id=1, source_target_pairs={{0,15},{1,0},{2,1},{3,2},{4,3},{5,4},{6,5},{7,6},{8,7},{9,8},{10,9... | collective-permute-start | bytes 1572872 | tf_op jit(solution)/shard_map/ppermute | solution.py:21
  31.9 2.4 %convert_element_type.175 = bf16[64,64,64]{2,1,0:T(8,128)(2,1)} reshape(bf16[2048,128]{1,0:T(8,128)(2,1)} %get-tuple-element.6) | data formatting | bytes 1048576 | tf_op jit(solution)/shard_map/convert_element_type | solution.py:227
  34.2 3.2 %fusion.24 = bf16[64,64,64]{2,0,1:T(8,128)(2,1)} fusion(bf16[64,64,64]{2,1,0:T(8,128)(2,1)} %convert_element_type.175), kind=kOutput, calls=%fused_computation.46 | convolution fusion | flops 33619968 | bytes 1048576 | tf_op jit(solution)/shard_map/ga,abc->gbc/dot_general | solution.py:49
  37.5 4.3 %multiply_convert_fusion.3 = bf16[64,64,64]{2,1,0:T(8,128)(2,1)} fusion(bf16[64,64,64]{2,0,1:T(8,128)(2,1)} %fusion.24, f32[64]{0:T(128)S(1)} %fusion.88, f32[64,64]{1,0:T(8,128)S(1)} %broadcast_add_fusion), kind=kOutput, calls=%fused_computation.20 | convolution fusion | flops 71172096 | bytes 1065216 | tf_op jit(solution)/shard_map/gc,abc->abg/dot_general | solution.py:49
  41.8 1.6 %mul.237 = f32[64,64,64]{2,1,0:T(8,128)} reshape(f32[2048,128]{1,0:T(8,128)S(1)} %get-tuple-element.9) | data formatting | bytes 2097152 | tf_op jit(solution)/shard_map/mul | solution.py:233
  43.5 2.2 %fusion.22 = bf16[64,64,64]{2,0,1:T(8,128)(2,1)S(1)} fusion(bf16[64,64,64]{2,1,0:T(8,128)(2,1)} %multiply_convert_fusion.3), kind=kOutput, calls=%fused_computation.44 | convolution fusion | flops 33619968 | bytes 1048576 | tf_op jit(solution)/shard_map/ga,abc->gbc/dot_general | solution.py:54
  45.7 2.6 %fusion.13 = f32[64,64,64]{2,1,0:T(8,128)} fusion(bf16[64,64,64]{2,0,1:T(8,128)(2,1)S(1)} %fusion.22), kind=kOutput, calls=%fused_computation.33 | convolution fusion | flops 67502080 | bytes 1572864 | tf_op jit(solution)/shard_map/gc,abc->abg/dot_general | solution.py:54
  48.3 4.3 %multiply_convert_fusion = bf16[64,64,64]{2,1,0:T(8,128)(2,1)S(1)} fusion(bf16[64,64,64]{2,1,0:T(8,128)(2,1)} %collective-permute-done.2, f32[64,64,64]{2,1,0:T(8,128)} %get-tuple-element.11, f32[64,64,64]{2,1,0:T(8,128)} %mul.237, f32[64,64,64]{2,1,0:T(8,128)} %fusion.13, f32[64,64,64]{2,1,0:T(8,128)S(1)} %mul.231), kind=kLoop, calls=%fused_computation.17 | loop fusion | flops 1835008 | bytes 5242880 | tf_op jit(solution)/shard_map/convert_element_type | solution.py:235
  52.6 1.3 %reshape_reshape.3.refs_0_ = bf16[16,128,128]{2,1,0:T(8,128)(2,1)} reshape(bf16[64,64,64]{2,1,0:T(8,128)(2,1)S(1)} %multiply_convert_fusion) | data formatting | bytes 1048576 | tf_op jit(solution)/shard_map/reshape;reshape | solution.py:238
  53.9 1.5 %reshape.98 = bf16[1,262144]{1,0:T(2,128)(2,1)} reshape(bf16[64,64,64]{2,1,0:T(8,128)(2,1)S(1)} %multiply_convert_fusion) | data formatting | bytes 1048576 | tf_op jit(solution)/shard_map/reshape | solution.py:235
  55.4 25.7 %to_slabs.1 = (bf16[16,128,128]{2,1,0:T(8,128)(2,1)}, bf16[16,128,128]{2,1,0:T(8,128)(2,1)}) custom-call(bf16[16,128,128]{2,1,0:T(8,128)(2,1)} %reshape_reshape.3.refs_0_, bf16[16,128,128]{2,1,0:T(8,128)(2,1)} %bitcast.51), custom_call_target="tpu_custom_call" | custom-call | bytes 20971520 | tf_op jit(solution)/shard_map/to_slabs/pallas_call | solution.py:115
  81.1 2.5 %convolution_bitcast_fusion.part_ref = f32[16,16]{1,0:T(8,128)} fusion(bf16[16,128,128]{2,1,0:T(8,128)(2,1)} %get-tuple-element.5, bf16[16,128,128]{2,1,0:T(8,128)(2,1)} %get-tuple-element.4), kind=kOutput, calls=%fused_computation.37 | convolution fusion | flops 8388608 | bytes 1049600 | tf_op jit(solution)/shard_map/dot_general | solution.py:241
  83.6 10.8 %summed.1 = f32[16,16]{1,0:T(8,128)} custom-call(f32[16,16]{1,0:T(8,128)} %convolution_bitcast_fusion.part_ref), custom_call_target="tpu_custom_call" | custom-call | tf_op jit(solution)/shard_map/summed/pallas_call | solution.py:169
  94.5 2.3 %fusion.1 = bf16[16,16384]{1,0:T(8,128)(2,1)} fusion(bf16[2,8,128,128]{3,2,1,0:T(8,128)(2,1)} %bitcast.52, f32[16,16]{1,0:T(8,128)} %summed.1), kind=kOutput, calls=%fused_computation.2 | convolution fusion | flops 9175552 | bytes 1049600 | tf_op jit(solution)/shard_map/dot_general | solution.py:246
  (6 shorter events, 1.0 us)
Async XLA Ops:
  3.1 13.2 %collective-permute-start = (bf16[2048,128]{1,0:T(8,128)(2,1)}, bf16[2048,128]{1,0:T(8,128)(2,1)S(1)}, u32[]{:S(2)}, u32[]{:S(2)}) collective-permute-start(bf16[2048,128]{1,0:T(8,128)(2,1)} %as_rows.2), channel_id=1, source_target_pairs={{0,1},{1,2},{2,3},{3,4},{4,5},{5,6},{6,7},{7,8},{8,9},{9,10},{10,1... | collective-permute-start | bytes 1572872 | tf_op jit(solution)/shard_map/ppermute | solution.py:21
  4.2 11.5 %collective-permute-start.1 = (bf16[1]{0:T(256)(128)(2,1)}, bf16[1]{0:T(256)(128)(2,1)}, u32[]{:S(2)}, u32[]{:S(2)}) collective-permute-start(bf16[1]{0:T(256)(128)(2,1)} %convert_element_type.186), channel_id=1, source_target_pairs={{0,1},{1,2},{2,3},{3,4},{4,5},{5,6},{6,7},{7,8},{8,9},{9,10},{10,1... | collective-permute-start | bytes 14 | tf_op jit(solution)/shard_map/ppermute | solution.py:21
  30.1 18.2 %collective-permute-start.2 = (bf16[64,64,64]{2,1,0:T(8,128)(2,1)}, bf16[64,64,64]{2,1,0:T(8,128)(2,1)}, u32[]{:S(2)}, u32[]{:S(2)}) collective-permute-start(bf16[64,64,64]{2,1,0:T(8,128)(2,1)} %get-tuple-element.10), channel_id=1, source_target_pairs={{0,15},{1,0},{2,1},{3,2},{4,3},{5,4},{6,5},{7,6},{8,7},{9,8},{10,9... | collective-permute-start | bytes 1572872 | tf_op jit(solution)/shard_map/ppermute | solution.py:21
where the time goes:
time: 97.3 us; the launch traced here: 96.8 us
  Pallas kernels  41.4 us (43%)
  matrix products  26.6 us (27%)
  local copies, waits for them, and re-layouts  8.77 us (9%)
  other arithmetic  6.8 us (7%)
  starting transfers between devices  5.87 us (6%)
  waiting for transfers between devices  5.39 us (6%)
  between operations  1.91 us (2%)
    pallas_call x1, Pallas kernels, to_slabs(): pl.pallas_call(functools.partial(slabs_body, count, number), out_shape=[j...  25.7 us
    dot_general x8, matrix products, screened_potential(): jnp.einsum(pattern, table, values, preferred_element_type=jnp.float32)  21.8 us
    pallas_call x1, Pallas kernels, summed(): pl.pallas_call(functools.partial(summed_body, count), out_shape=jax.Shape...  10.8 us
    ppermute x3, starting transfers between devices, passed_along(): return lax.ppermute(value, axis, pairs)  5.87 us
    ppermute x3, waiting for transfers between devices, passed_along(): return lax.ppermute(value, axis, pairs)  5.39 us
    pallas_call x2, Pallas kernels, as_rows(): pl.pallas_call(functools.partial(rows_body, CHUNK), out_shape=[jax.ShapeD...  4.85 us
    convert_element_type x1, other arithmetic, local(): exchange = (-FRACTION * accumulated).astype(jnp.bfloat16).reshape(1, cells)  4.26 us
    dot_general x1, matrix products, local(): lax.dot_general(grid_exchange, grid_trial, (((1,), (1,)), ((), ())), pref...  2.51 us
  transfers between devices with their start and end apart: 3, of which 1 were waited for; matrix products, arithmetic and copies ran while one was open for 17% of the time, Pallas kernels for 2%

commit v1 on v0

--- a/solution.py
+++ b/solution.py
@@ -215,13 +215,17 @@
     cells = orbitals.shape[1]
     extent = NG
     table = cas_table(extent)
-    kernel = screened_kernel(extent)
+    kernel = lax.optimization_barrier(screened_kernel(extent))
     cube = (extent, extent, extent)
     fill = occupations.astype(jnp.bfloat16)
 
     (lined,) = as_rows(orbitals)
     (trial_rows,) = as_rows(trial)
     visitor, visitor_fill = passed_along((lined, fill), "band", 1)
+    slab = (count, cells // count // 128, 128)
+    grid_trial = lax.all_to_all(
+        trial_rows.reshape(slab), "band", split_axis=0, concat_axis=0, tiled=True
+    )
     own = lined.reshape(cube).astype(jnp.float32)
     own_weighted = own * fill[0].astype(jnp.float32)
     own_potential = screened_potential((own * own).astype(jnp.bfloat16), table, kernel)
@@ -234,8 +238,7 @@
     accumulated = accumulated + carried.astype(jnp.float32)
     exchange = (-FRACTION * accumulated).astype(jnp.bfloat16).reshape(1, cells)
 
-    slab = (count, cells // count // 128, 128)
-    grid_exchange, grid_trial = to_slabs((exchange.reshape(slab), trial_rows.reshape(slab)), 1)
+    (grid_exchange,) = to_slabs((exchange.reshape(slab),), 1)
     grid_exchange = grid_exchange.reshape(count, -1)
     grid_trial = grid_trial.reshape(count, -1)
     part = lax.dot_general(

time: 97.3 us -> 99.8 us (1.026)
  Pallas kernels: 41.4 us -> 29.1 us
  starting transfers between devices: 5.87 us -> 17.8 us
  waiting for transfers between devices: 5.39 us -> 0.01 us
  matrix products: 26.6 us -> 31.3 us
  local copies, waits for them, and re-layouts: 8.77 us -> 10.8 us
  other arithmetic: 6.8 us -> 7.87 us
    pallas_call x1, Pallas kernels: 25.7 us -> 13.6 us  [to_slabs(): pl.pallas_call(functools.partial(slabs_body, count, number), out_shape=[j...]
    all_to_all x0 -> x1, starting transfers between devices: none -> 9.55 us  [local(): lax.all_to_all(trial_rows.reshape(slab), 'band', split_axis=0, concat_axi...]
    ppermute x3, waiting for transfers between devices: 5.39 us -> 0.01 us  [passed_along(): return lax.ppermute(value, axis, pairs)]
    dot_general x8, matrix products: 21.8 us -> 26.5 us  [screened_potential(): jnp.einsum(pattern, table, values, preferred_element_type=jnp.float32)]
    ppermute x3, starting transfers between devices: 5.87 us -> 8.28 us  [passed_along(): return lax.ppermute(value, axis, pairs)]
    convert_element_type x1, local copies, waits for them, and re-layouts: 0.4 us -> 2.38 us  [local(): (own * other).astype(jnp.bfloat16)]
  transfers between devices with their start and end apart: 3 -> 4, of which waited for: 1 -> 0; matrix products, arithmetic and copies ran while one was open for 17% -> 46% of each run, Pallas kernels for 2% -> 16%
where the time goes in v1:
time: 99.8 us; the launch traced here: 99 us
  matrix products  31.3 us (31%)
  Pallas kernels  29.1 us (29%)
  starting transfers between devices  17.8 us (18%)
  local copies, waits for them, and re-layouts  10.8 us (11%)
  other arithmetic  7.87 us (8%)
  between operations  2.05 us (2%)
    dot_general x8, matrix products, screened_potential(): jnp.einsum(pattern, table, values, preferred_element_type=jnp.float32)  26.5 us
    pallas_call x1, Pallas kernels, to_slabs(): pl.pallas_call(functools.partial(slabs_body, count, number), out_shape=[j...  13.6 us
    pallas_call x1, Pallas kernels, summed(): pl.pallas_call(functools.partial(summed_body, count), out_shape=jax.Shape...  10.6 us
    all_to_all x1, starting transfers between devices, local(): lax.all_to_all(trial_rows.reshape(slab), 'band', split_axis=0, concat_axi...  9.55 us
    ppermute x3, starting transfers between devices, passed_along(): return lax.ppermute(value, axis, pairs)  8.28 us
    pallas_call x2, Pallas kernels, as_rows(): pl.pallas_call(functools.partial(rows_body, CHUNK), out_shape=[jax.ShapeD...  4.91 us
    convert_element_type x1, other arithmetic, local(): exchange = (-FRACTION * accumulated).astype(jnp.bfloat16).reshape(1, cells)  4.26 us
    convert_element_type x1, other arithmetic, local(): (own * own).astype(jnp.bfloat16)  2.63 us
  transfers between devices with their start and end apart: 4, of which 0 were waited for; matrix products, arithmetic and copies ran while one was open for 46% of the time, Pallas kernels for 16%

profile of v1, /device:TPU:0, one launch (start us, length us, event | category | flops | bytes accessed | tf_op | source)
XLA Modules:
  0.0 99.0 jit_solution(4791812408119601599)
XLA Ops:
  0.6 2.4 %as_rows.2 = bf16[2048,128]{1,0:T(8,128)(2,1)} custom-call(bf16[1,262144]{1,0:T(2,128)(2,1)} %refs_0_.2), custom_call_target="tpu_custom_call" | custom-call | bytes 4194304 | tf_op jit(solution)/shard_map/as_rows/pallas_call | solution.py:201
  4.2 3.5 %collective-permute-start.1 = (bf16[1]{0:T(256)(128)(2,1)}, bf16[1]{0:T(256)(128)(2,1)}, u32[]{:S(2)}, u32[]{:S(2)}) collective-permute-start(bf16[1]{0:T(256)(128)(2,1)} %convert_element_type.184), channel_id=1, source_target_pairs={{0,1},{1,2},{2,3},{3,4},{4,5},{5,6},{6,7},{7,8},{8,9},{9,10},{10,1... | collective-permute-start | bytes 14 | tf_op jit(solution)/shard_map/ppermute | solution.py:21
  7.7 2.5 %as_rows.3 = bf16[2048,128]{1,0:T(8,128)(2,1)} custom-call(bf16[1,262144]{1,0:T(2,128)(2,1)} %refs_0_.3), custom_call_target="tpu_custom_call" | custom-call | bytes 4194304 | tf_op jit(solution)/shard_map/as_rows/pallas_call | solution.py:201
  10.2 9.6 %all-to-all-start = ((bf16[16,128,128]{2,1,0:T(8,128)(2,1)}), bf16[16,128,128]{2,1,0:T(8,128)(2,1)}, u32[]{:S(2)}, u32[]{:S(2)}) async-start(bf16[16,128,128]{2,1,0:T(8,128)(2,1)} %bitcast.51), calls=%async_computation | async-start | bytes 1048576 | tf_op jit(solution)/shard_map/all_to_all | solution.py:226
  21.4 2.6 %fusion.16 = (bf16[2048,128]{1,0:T(8,128)(2,1)}, f32[2048,128]{1,0:T(8,128)}, bf16[2048,128]{1,0:T(8,128)(2,1)}, f32[2048,128]{1,0:T(8,128)S(1)}) fusion(bf16[2048,128]{1,0:T(8,128)(2,1)} %as_rows.2, f32[]{:T(128)S(6)} %convert.2, bf16[2048,128]{1,0:T(8,128)(2,1)} %collective-permute-done, f32[]{:T(128)S(6)} %convert.3), kind=kLoop, calls=%fused_computation.38 | loop fusion | flops 2097152 | bytes 4194312 | tf_op jit(solution)/shard_map/convert_element_type | solution.py:231
  24.1 2.4 %convert_element_type.189 = bf16[64,64,64]{2,1,0:T(8,128)(2,1)} reshape(bf16[2048,128]{1,0:T(8,128)(2,1)} %get-tuple-element.4) | data formatting | bytes 1048576 | tf_op jit(solution)/shard_map/convert_element_type | solution.py:235
  26.4 3.2 %fusion.20 = bf16[64,64,64]{2,0,1:T(8,128)(2,1)} fusion(bf16[64,64,64]{2,1,0:T(8,128)(2,1)} %convert_element_type.189), kind=kOutput, calls=%fused_computation.42 | convolution fusion | flops 33619968 | bytes 1048576 | tf_op jit(solution)/shard_map/ga,abc->gbc/dot_general | solution.py:49
  29.7 3.5 %multiply_convert_fusion.2 = bf16[64,64,64]{2,1,0:T(8,128)(2,1)} fusion(f32[64,64,64]{2,1,0:T(8,128)S(1)} %fusion.6, bf16[64,64,64]{2,0,1:T(8,128)(2,1)} %fusion.20), kind=kOutput, calls=%fused_computation.19 | convolution fusion | flops 68550656 | bytes 2097152 | tf_op jit(solution)/shard_map/gc,abc->abg/dot_general | solution.py:49
  33.2 3.2 %fusion.18 = bf16[64,64,64]{2,0,1:T(8,128)(2,1)} fusion(bf16[64,64,64]{2,1,0:T(8,128)(2,1)} %multiply_convert_fusion.2), kind=kOutput, calls=%fused_computation.40 | convolution fusion | flops 33619968 | bytes 1048576 | tf_op jit(solution)/shard_map/ga,abc->gbc/dot_general | solution.py:54
  36.4 1.6 %mul.223 = f32[64,64,64]{2,1,0:T(8,128)S(1)} reshape(f32[2048,128]{1,0:T(8,128)} %get-tuple-element.3) | data formatting | bytes 2097152 | tf_op jit(solution)/shard_map/mul | solution.py:230
  38.0 4.2 %multiply_convert_fusion.1 = (bf16[64,64,64]{2,1,0:T(8,128)(2,1)}, f32[64,64,64]{2,1,0:T(8,128)}) fusion(f32[64,64,64]{2,1,0:T(8,128)S(1)} %mul.223, bf16[64,64,64]{2,0,1:T(8,128)(2,1)} %fusion.18), kind=kOutput, calls=%fused_computation.18 | convolution fusion | flops 68026368 | bytes 3145728 | tf_op jit(solution)/shard_map/gc,abc->abg/dot_general | solution.py:54
  42.2 4.3 %collective-permute-start.2 = (bf16[64,64,64]{2,1,0:T(8,128)(2,1)}, bf16[64,64,64]{2,1,0:T(8,128)(2,1)}, u32[]{:S(2)}, u32[]{:S(2)}) collective-permute-start(bf16[64,64,64]{2,1,0:T(8,128)(2,1)} %get-tuple-element.6), channel_id=1, source_target_pairs={{0,15},{1,0},{2,1},{3,2},{4,3},{5,4},{6,5},{7,6},{8,7},{9,8},{10,9... | collective-permute-start | bytes 1572872 | tf_op jit(solution)/shard_map/ppermute | solution.py:21
  46.5 2.4 %convert_element_type.173 = bf16[64,64,64]{2,1,0:T(8,128)(2,1)} reshape(bf16[2048,128]{1,0:T(8,128)(2,1)} %get-tuple-element.2) | data formatting | bytes 1048576 | tf_op jit(solution)/shard_map/convert_element_type | solution.py:231
  48.9 3.2 %fusion.24 = bf16[64,64,64]{2,0,1:T(8,128)(2,1)} fusion(bf16[64,64,64]{2,1,0:T(8,128)(2,1)} %convert_element_type.173), kind=kOutput, calls=%fused_computation.46 | convolution fusion | flops 33619968 | bytes 1048576 | tf_op jit(solution)/shard_map/ga,abc->gbc/dot_general | solution.py:49
  52.1 4.3 %multiply_convert_fusion.3 = bf16[64,64,64]{2,1,0:T(8,128)(2,1)} fusion(f32[64,64,64]{2,1,0:T(8,128)} %copy-done, bf16[64,64,64]{2,0,1:T(8,128)(2,1)} %fusion.24), kind=kOutput, calls=%fused_computation.20 | convolution fusion | flops 68550656 | bytes 2097152 | tf_op jit(solution)/shard_map/gc,abc->abg/dot_general | solution.py:49
  56.3 1.7 %mul.229 = f32[64,64,64]{2,1,0:T(8,128)} reshape(f32[2048,128]{1,0:T(8,128)S(1)} %get-tuple-element.5) | data formatting | bytes 2097152 | tf_op jit(solution)/shard_map/mul | solution.py:237
  58.0 2.2 %fusion.22 = bf16[64,64,64]{2,0,1:T(8,128)(2,1)S(1)} fusion(bf16[64,64,64]{2,1,0:T(8,128)(2,1)} %multiply_convert_fusion.3), kind=kOutput, calls=%fused_computation.44 | convolution fusion | flops 33619968 | bytes 1048576 | tf_op jit(solution)/shard_map/ga,abc->gbc/dot_general | solution.py:54
  60.3 2.6 %fusion.13 = f32[64,64,64]{2,1,0:T(8,128)} fusion(bf16[64,64,64]{2,0,1:T(8,128)(2,1)S(1)} %fusion.22), kind=kOutput, calls=%fused_computation.33 | convolution fusion | flops 67502080 | bytes 1572864 | tf_op jit(solution)/shard_map/gc,abc->abg/dot_general | solution.py:54
  62.9 4.3 %multiply_convert_fusion = bf16[64,64,64]{2,1,0:T(8,128)(2,1)S(1)} fusion(bf16[64,64,64]{2,1,0:T(8,128)(2,1)} %collective-permute-done.2, f32[64,64,64]{2,1,0:T(8,128)} %get-tuple-element.7, f32[64,64,64]{2,1,0:T(8,128)} %mul.229, f32[64,64,64]{2,1,0:T(8,128)} %fusion.13, f32[64,64,64]{2,1,0:T(8,128)S(1)} %mul.223), kind=kLoop, calls=%fused_computation.17 | loop fusion | flops 1835008 | bytes 5242880 | tf_op jit(solution)/shard_map/convert_element_type | solution.py:239
  68.4 1.5 %reshape.98 = bf16[1,262144]{1,0:T(2,128)(2,1)} reshape(bf16[64,64,64]{2,1,0:T(8,128)(2,1)S(1)} %multiply_convert_fusion) | data formatting | bytes 1048576 | tf_op jit(solution)/shard_map/reshape | solution.py:239
  70.0 13.6 %to_slabs.1 = bf16[16,128,128]{2,1,0:T(8,128)(2,1)} custom-call(bf16[16,128,128]{2,1,0:T(8,128)(2,1)} %reshape_reshape.3.refs_0_), custom_call_target="tpu_custom_call" | custom-call | bytes 10485760 | tf_op jit(solution)/shard_map/to_slabs/pallas_call | solution.py:115
  83.6 2.5 %convolution_bitcast_fusion.part_ref = f32[16,16]{1,0:T(8,128)} fusion(bf16[16,128,128]{2,1,0:T(8,128)(2,1)} %all-to-all-done, bf16[16,128,128]{2,1,0:T(8,128)(2,1)} %to_slabs.1), kind=kOutput, calls=%fused_computation.37 | convolution fusion | flops 8388608 | bytes 1049600 | tf_op jit(solution)/shard_map/dot_general | solution.py:244
  86.1 10.6 %summed.1 = f32[16,16]{1,0:T(8,128)} custom-call(f32[16,16]{1,0:T(8,128)} %convolution_bitcast_fusion.part_ref), custom_call_target="tpu_custom_call" | custom-call | tf_op jit(solution)/shard_map/summed/pallas_call | solution.py:169
  96.7 2.3 %fusion.1 = bf16[16,16384]{1,0:T(8,128)(2,1)} fusion(bf16[2,8,128,128]{3,2,1,0:T(8,128)(2,1)} %bitcast.52, f32[16,16]{1,0:T(8,128)} %summed.1), kind=kOutput, calls=%fused_computation.2 | convolution fusion | flops 9175552 | bytes 1049600 | tf_op jit(solution)/shard_map/dot_general | solution.py:249
  (11 shorter events, 2.8 us)
Async XLA Ops:
  3.1 18.4 %collective-permute-start = (bf16[2048,128]{1,0:T(8,128)(2,1)}, bf16[2048,128]{1,0:T(8,128)(2,1)}, u32[]{:S(2)}, u32[]{:S(2)}) collective-permute-start(bf16[2048,128]{1,0:T(8,128)(2,1)} %as_rows.2), channel_id=1, source_target_pairs={{0,1},{1,2},{2,3},{3,4},{4,5},{5,6},{6,7},{7,8},{8,9},{9,10},{10,1... | collective-permute-start | bytes 1572872 | tf_op jit(solution)/shard_map/ppermute | solution.py:21
  4.2 16.5 %collective-permute-start.1 = (bf16[1]{0:T(256)(128)(2,1)}, bf16[1]{0:T(256)(128)(2,1)}, u32[]{:S(2)}, u32[]{:S(2)}) collective-permute-start(bf16[1]{0:T(256)(128)(2,1)} %convert_element_type.184), channel_id=1, source_target_pairs={{0,1},{1,2},{2,3},{3,4},{4,5},{5,6},{6,7},{7,8},{8,9},{9,10},{10,1... | collective-permute-start | bytes 14 | tf_op jit(solution)/shard_map/ppermute | solution.py:21
  10.2 73.4 %all-to-all-start = ((bf16[16,128,128]{2,1,0:T(8,128)(2,1)}), bf16[16,128,128]{2,1,0:T(8,128)(2,1)}, u32[]{:S(2)}, u32[]{:S(2)}) async-start(bf16[16,128,128]{2,1,0:T(8,128)(2,1)} %bitcast.51), calls=%async_computation | async-start | bytes 1048576 | tf_op jit(solution)/shard_map/all_to_all | solution.py:226
  20.7 9.0 %copy-start = (f32[64,64,64]{2,1,0:T(8,128)}, f32[64,64,64]{2,1,0:T(8,128)S(1)}, u32[]{:S(2)}) copy-start(f32[64,64,64]{2,1,0:T(8,128)S(1)} %fusion.6) | copy-start | bytes 3145732
  42.2 20.7 %collective-permute-start.2 = (bf16[64,64,64]{2,1,0:T(8,128)(2,1)}, bf16[64,64,64]{2,1,0:T(8,128)(2,1)}, u32[]{:S(2)}, u32[]{:S(2)}) collective-permute-start(bf16[64,64,64]{2,1,0:T(8,128)(2,1)} %get-tuple-element.6), channel_id=1, source_target_pairs={{0,15},{1,0},{2,1},{3,2},{4,3},{5,4},{6,5},{7,6},{8,7},{9,8},{10,9... | collective-permute-start | bytes 1572872 | tf_op jit(solution)/shard_map/ppermute | solution.py:21

commit v2 on v0

--- a/solution.py
+++ b/solution.py
@@ -12,6 +12,7 @@
 FRACTION = 0.25
 OMEGA = 1.0
 CHUNK = 2048
+TAG = 16
 MESH = pl.DeviceIdType.MESH
 
 
@@ -195,6 +196,23 @@
             rows[out, :] = wide.astype(rows.dtype)
 
 
+def tagged_body(chunk, line, tag, rows):
+    rows_body(chunk, line, rows)
+    full = line.shape[1] // 128
+    rows[full:, :] = jnp.broadcast_to(tag[...], (TAG, 128)).astype(rows.dtype)
+
+
+def tagged_rows(line, tag):
+    cells = line.shape[1]
+    return pl.pallas_call(
+        functools.partial(tagged_body, CHUNK),
+        out_shape=jax.ShapeDtypeStruct((cells // 128 + TAG, 128), line.dtype),
+        in_specs=[pl.BlockSpec(memory_space=pltpu.VMEM)] * 2,
+        out_specs=pl.BlockSpec(memory_space=pltpu.VMEM),
+        name="tagged_rows",
+    )(line, tag)
+
+
 def as_rows(*lines):
     number = len(lines)
     cells = lines[0].shape[1]
@@ -219,10 +237,13 @@
     cube = (extent, extent, extent)
     fill = occupations.astype(jnp.bfloat16)
 
-    (lined,) = as_rows(orbitals)
+    tag = jnp.broadcast_to(occupations.astype(jnp.float32).reshape(1, 1), (1, 128))
+    lined = tagged_rows(orbitals, tag)
     (trial_rows,) = as_rows(trial)
-    visitor, visitor_fill = passed_along((lined, fill), "band", 1)
-    own = lined.reshape(cube).astype(jnp.float32)
+    passed = passed_along(lined, "band", 1)
+    full = cells // 128
+    visitor, visitor_fill = passed[:full], passed[full, :1]
+    own = lined[:full].reshape(cube).astype(jnp.float32)
     own_weighted = own * fill[0].astype(jnp.float32)
     own_potential = screened_potential((own * own).astype(jnp.bfloat16), table, kernel)
     accumulated = own_potential * own_weighted

time: 97.3 us -> 97.4 us (level)
  starting transfers between devices: 5.87 us -> 0.5 us
  waiting for transfers between devices: 5.39 us -> 9.6 us
  local copies, waits for them, and re-layouts: 8.77 us -> 9.81 us
    ppermute x3 -> x2, starting transfers between devices: 5.87 us -> 0.5 us  [passed_along(): return lax.ppermute(value, axis, pairs)]
    ppermute x3 -> x2, waiting for transfers between devices: 5.39 us -> 9.6 us  [passed_along(): return lax.ppermute(value, axis, pairs)]
    pallas_call x0 -> x1, Pallas kernels: none -> 2.44 us  [tagged_rows(): pl.pallas_call(functools.partial(tagged_body, CHUNK), out_shape=jax.Shape...]
    pallas_call x2 -> x1, Pallas kernels: 4.85 us -> 2.42 us  [as_rows(): pl.pallas_call(functools.partial(rows_body, CHUNK), out_shape=[jax.ShapeD...]
  transfers between devices with their start and end apart: 3 -> 2, of which waited for: 1 -> 1; matrix products, arithmetic and copies ran while one was open for 17% -> 17% of each run, Pallas kernels for 2% -> 2%
where the time goes in v2:
time: 97.4 us; the launch traced here: 96.8 us
  Pallas kernels  41.5 us (43%)
  matrix products  26.6 us (27%)
  local copies, waits for them, and re-layouts  9.81 us (10%)
  waiting for transfers between devices  9.6 us (10%)
  other arithmetic  6.8 us (7%)
  between operations  1.98 us (2%)
    pallas_call x1, Pallas kernels, to_slabs(): pl.pallas_call(functools.partial(slabs_body, count, number), out_shape=[j...  25.8 us
    dot_general x8, matrix products, screened_potential(): jnp.einsum(pattern, table, values, preferred_element_type=jnp.float32)  21.8 us
    pallas_call x1, Pallas kernels, summed(): pl.pallas_call(functools.partial(summed_body, count), out_shape=jax.Shape...  10.9 us
    ppermute x2, waiting for transfers between devices, passed_along(): return lax.ppermute(value, axis, pairs)  9.6 us
    convert_element_type x1, other arithmetic, local(): exchange = (-FRACTION * accumulated).astype(jnp.bfloat16).reshape(1, cells)  4.26 us
    dot_general x1, matrix products, local(): lax.dot_general(grid_exchange, grid_trial, (((1,), (1,)), ((), ())), pref...  2.51 us
    convert_element_type x1, other arithmetic, local(): (own * own).astype(jnp.bfloat16)  2.46 us
    pallas_call x1, Pallas kernels, tagged_rows(): pl.pallas_call(functools.partial(tagged_body, CHUNK), out_shape=jax.Shape...  2.44 us
  transfers between devices with their start and end apart: 2, of which 1 were waited for; matrix products, arithmetic and copies ran while one was open for 17% of the time, Pallas kernels for 2%

profile of v2, /device:TPU:0, one launch (start us, length us, event | category | flops | bytes accessed | tf_op | source)
XLA Modules:
  0.0 96.8 jit_solution(7726710729159182390)
XLA Ops:
  1.3 0.5 broadcast_in_dim.20.tag
  1.8 2.4 %tagged_rows.1 = bf16[2064,128]{1,0:T(8,128)(2,1)} custom-call(bf16[1,262144]{1,0:T(2,128)(2,1)} %line.1, f32[1,128]{1,0:T(1,128)} %broadcast_in_dim.20.tag), custom_call_target="tpu_custom_call" | custom-call | tf_op jit(solution)/shard_map/tagged_rows/pallas_call | solution.py:207
  4.7 2.4 %as_rows.1 = bf16[2048,128]{1,0:T(8,128)(2,1)} custom-call(bf16[1,262144]{1,0:T(2,128)(2,1)} %refs_0_.1), custom_call_target="tpu_custom_call" | custom-call | bytes 4194304 | tf_op jit(solution)/shard_map/as_rows/pallas_call | solution.py:219
  7.2 9.6 %collective-permute-done = bf16[2064,128]{1,0:T(8,128)(2,1)S(1)} collective-permute-done((bf16[2064,128]{1,0:T(8,128)(2,1)}, bf16[2064,128]{1,0:T(8,128)(2,1)S(1)}, u32[]{:S(2)}, u32[]{:S(2)}) %collective-permute-start) | collective-permute-done | bytes 528416 | tf_op jit(solution)/shard_map/ppermute | solution.py:22
  16.8 0.5 slice.14
  18.0 2.5 %fusion.16 = (bf16[2048,128]{1,0:T(8,128)(2,1)}, bf16[2048,128]{1,0:T(8,128)(2,1)S(1)}, f32[2048,128]{1,0:T(8,128)S(1)}, f32[2048,128]{1,0:T(8,128)}) fusion(bf16[2064,128]{1,0:T(8,128)(2,1)} %tagged_rows.1, bf16[2064,128]{1,0:T(8,128)(2,1)S(1)} %collective-permute-done, f32[]{:T(128)S(6)} %convert.3, f32[]{:T(128)S(6)} %convert.2), kind=kLoop, calls=%fused_computation.38 | loop fusion | flops 2097152 | bytes 4194312 | tf_op jit(solution)/shard_map/convert_element_type | solution.py:248
  20.9 1.0 %fusion.20 = bf16[64,64,64]{2,0,1:T(8,128)(2,1)S(1)} fusion(bf16[64,64,64]{2,1,0:T(8,128)(2,1)S(1)} %convert_element_type.195), kind=kOutput, calls=%fused_computation.42 | convolution fusion | flops 33619968 | bytes 1048576 | tf_op jit(solution)/shard_map/ga,abc->gbc/dot_general | solution.py:50
  21.9 2.2 %multiply_convert_fusion.2 = bf16[64,64,64]{2,1,0:T(8,128)(2,1)S(1)} fusion(bf16[64,64,64]{2,0,1:T(8,128)(2,1)S(1)} %fusion.20, f32[64]{0:T(128)S(1)} %fusion.88, f32[64,64]{1,0:T(8,128)S(1)} %broadcast_add_fusion), kind=kOutput, calls=%fused_computation.19 | convolution fusion | flops 71172096 | bytes 1065216 | tf_op jit(solution)/shard_map/gc,abc->abg/dot_general | solution.py:50
  24.0 2.0 %fusion.18 = bf16[64,64,64]{2,0,1:T(8,128)(2,1)} fusion(bf16[64,64,64]{2,1,0:T(8,128)(2,1)S(1)} %multiply_convert_fusion.2), kind=kOutput, calls=%fused_computation.40 | convolution fusion | flops 33619968 | bytes 1048576 | tf_op jit(solution)/shard_map/ga,abc->gbc/dot_general | solution.py:55
  26.1 1.6 %mul.231 = f32[64,64,64]{2,1,0:T(8,128)S(1)} reshape(f32[2048,128]{1,0:T(8,128)} %get-tuple-element.9) | data formatting | bytes 2097152 | tf_op jit(solution)/shard_map/mul | solution.py:247
  27.6 4.2 %multiply_convert_fusion.1 = (bf16[64,64,64]{2,1,0:T(8,128)(2,1)}, f32[64,64,64]{2,1,0:T(8,128)}) fusion(f32[64,64,64]{2,1,0:T(8,128)S(1)} %mul.231, bf16[64,64,64]{2,0,1:T(8,128)(2,1)} %fusion.18), kind=kOutput, calls=%fused_computation.18 | convolution fusion | flops 68026368 | bytes 3145728 | tf_op jit(solution)/shard_map/gc,abc->abg/dot_general | solution.py:55
  31.8 2.4 %convert_element_type.179 = bf16[64,64,64]{2,1,0:T(8,128)(2,1)} reshape(bf16[2048,128]{1,0:T(8,128)(2,1)} %get-tuple-element.6) | data formatting | bytes 1048576 | tf_op jit(solution)/shard_map/convert_element_type | solution.py:248
  34.2 3.2 %fusion.24 = bf16[64,64,64]{2,0,1:T(8,128)(2,1)} fusion(bf16[64,64,64]{2,1,0:T(8,128)(2,1)} %convert_element_type.179), kind=kOutput, calls=%fused_computation.46 | convolution fusion | flops 33619968 | bytes 1048576 | tf_op jit(solution)/shard_map/ga,abc->gbc/dot_general | solution.py:50
  37.4 4.4 %multiply_convert_fusion.3 = bf16[64,64,64]{2,1,0:T(8,128)(2,1)} fusion(bf16[64,64,64]{2,0,1:T(8,128)(2,1)} %fusion.24, f32[64]{0:T(128)S(1)} %fusion.88, f32[64,64]{1,0:T(8,128)S(1)} %broadcast_add_fusion), kind=kOutput, calls=%fused_computation.20 | convolution fusion | flops 71172096 | bytes 1065216 | tf_op jit(solution)/shard_map/gc,abc->abg/dot_general | solution.py:50
  41.8 1.6 %mul.237 = f32[64,64,64]{2,1,0:T(8,128)} reshape(f32[2048,128]{1,0:T(8,128)S(1)} %get-tuple-element.8) | data formatting | bytes 2097152 | tf_op jit(solution)/shard_map/mul | solution.py:254
  43.4 2.2 %fusion.22 = bf16[64,64,64]{2,0,1:T(8,128)(2,1)S(1)} fusion(bf16[64,64,64]{2,1,0:T(8,128)(2,1)} %multiply_convert_fusion.3), kind=kOutput, calls=%fused_computation.44 | convolution fusion | flops 33619968 | bytes 1048576 | tf_op jit(solution)/shard_map/ga,abc->gbc/dot_general | solution.py:55
  45.6 2.6 %fusion.13 = f32[64,64,64]{2,1,0:T(8,128)} fusion(bf16[64,64,64]{2,0,1:T(8,128)(2,1)S(1)} %fusion.22), kind=kOutput, calls=%fused_computation.33 | convolution fusion | flops 67502080 | bytes 1572864 | tf_op jit(solution)/shard_map/gc,abc->abg/dot_general | solution.py:55
  48.3 4.3 %multiply_convert_fusion = bf16[64,64,64]{2,1,0:T(8,128)(2,1)S(1)} fusion(bf16[64,64,64]{2,1,0:T(8,128)(2,1)} %collective-permute-done.1, f32[64,64,64]{2,1,0:T(8,128)} %get-tuple-element.11, f32[64,64,64]{2,1,0:T(8,128)} %mul.237, f32[64,64,64]{2,1,0:T(8,128)} %fusion.13, f32[64,64,64]{2,1,0:T(8,128)S(1)} %mul.231), kind=kLoop, calls=%fused_computation.17 | loop fusion | flops 1835008 | bytes 5242880 | tf_op jit(solution)/shard_map/convert_element_type | solution.py:256
  52.5 1.3 %reshape_reshape.3.refs_0_ = bf16[16,128,128]{2,1,0:T(8,128)(2,1)} reshape(bf16[64,64,64]{2,1,0:T(8,128)(2,1)S(1)} %multiply_convert_fusion) | data formatting | bytes 1048576 | tf_op jit(solution)/shard_map/reshape;reshape | solution.py:259
  53.8 1.5 %reshape.102 = bf16[1,262144]{1,0:T(2,128)(2,1)} reshape(bf16[64,64,64]{2,1,0:T(8,128)(2,1)S(1)} %multiply_convert_fusion) | data formatting | bytes 1048576 | tf_op jit(solution)/shard_map/reshape | solution.py:256
  55.3 25.8 %to_slabs.1 = (bf16[16,128,128]{2,1,0:T(8,128)(2,1)}, bf16[16,128,128]{2,1,0:T(8,128)(2,1)}) custom-call(bf16[16,128,128]{2,1,0:T(8,128)(2,1)} %reshape_reshape.3.refs_0_, bf16[16,128,128]{2,1,0:T(8,128)(2,1)} %bitcast.52), custom_call_target="tpu_custom_call" | custom-call | bytes 20971520 | tf_op jit(solution)/shard_map/to_slabs/pallas_call | solution.py:116
  81.2 2.5 %convolution_bitcast_fusion.part_ref = f32[16,16]{1,0:T(8,128)} fusion(bf16[16,128,128]{2,1,0:T(8,128)(2,1)} %get-tuple-element.5, bf16[16,128,128]{2,1,0:T(8,128)(2,1)} %get-tuple-element.4), kind=kOutput, calls=%fused_computation.37 | convolution fusion | flops 8388608 | bytes 1049600 | tf_op jit(solution)/shard_map/dot_general | solution.py:262
  83.7 10.9 %summed.1 = f32[16,16]{1,0:T(8,128)} custom-call(f32[16,16]{1,0:T(8,128)} %convolution_bitcast_fusion.part_ref), custom_call_target="tpu_custom_call" | custom-call | tf_op jit(solution)/shard_map/summed/pallas_call | solution.py:170
  94.5 2.3 %fusion.1 = bf16[16,16384]{1,0:T(8,128)(2,1)} fusion(bf16[2,8,128,128]{3,2,1,0:T(8,128)(2,1)} %bitcast.53, f32[16,16]{1,0:T(8,128)} %summed.1), kind=kOutput, calls=%fused_computation.2 | convolution fusion | flops 9175552 | bytes 1049600 | tf_op jit(solution)/shard_map/dot_general | solution.py:267
  (6 shorter events, 1.0 us)
Async XLA Ops:
  4.2 12.6 %collective-permute-start = (bf16[2064,128]{1,0:T(8,128)(2,1)}, bf16[2064,128]{1,0:T(8,128)(2,1)S(1)}, u32[]{:S(2)}, u32[]{:S(2)}) collective-permute-start(bf16[2064,128]{1,0:T(8,128)(2,1)} %tagged_rows.1), channel_id=1, source_target_pairs={{0,1},{1,2},{2,3},{3,4},{4,5},{5,6},{6,7},{7,8},{8,9},{9,10},{10,1... | collective-permute-start | bytes 1585160 | tf_op jit(solution)/shard_map/ppermute | solution.py:22
  31.8 16.5 %collective-permute-start.1 = (bf16[64,64,64]{2,1,0:T(8,128)(2,1)}, bf16[64,64,64]{2,1,0:T(8,128)(2,1)}, u32[]{:S(2)}, u32[]{:S(2)}) collective-permute-start(bf16[64,64,64]{2,1,0:T(8,128)(2,1)} %get-tuple-element.10), channel_id=1, source_target_pairs={{0,15},{1,0},{2,1},{3,2},{4,3},{5,4},{6,5},{7,6},{8,7},{9,8},{10,9... | collective-permute-start | bytes 1572872 | tf_op jit(solution)/shard_map/ppermute | solution.py:22
